TPU v7x, 32 devices: a whole 2x2x4 slice. The times are simulated.
32 devices in a mesh: dp: 8 (over y, x, core), seq: 4 (over z).
Axes of the slice: x: 2, y: 2, z: 4, core: 2. Of those that a mesh axis runs over, the one named last changes fastest.
Arguments:
- tokens: bfloat16 [8, 1024, 1024], P('dp', 'seq'), may hold values from -6 to 6
- segments: int32 [8, 1024], P('dp'), may hold values from 0 to 6, as said below
- w_qkv: bfloat16 [1024, 3072], P('dp'), may hold values from -0.1875 to 0.1875
- w_attn_out: bfloat16 [1024, 1024], P('dp'), may hold values from -0.1875 to 0.1875
- w_in: bfloat16 [1024, 8192], P('dp'), may hold values from -0.1875 to 0.1875
- w_down: bfloat16 [4096, 1024], P('dp'), may hold values from -0.09375 to 0.09375
- s_qk: float32 [1024], replicated, may hold values from 1 to 1.8
- s_u: float32 [4096], replicated, may hold values from 0.5 to 2
- s_v: float32 [4096], replicated, may hold values from 0.5 to 2
- alpha_attn: float32 [1024], replicated, may hold values from 0.05 to 0.4
- alpha_mlp: float32 [1024], replicated, may hold values from 0.05 to 0.4
- cotangent: bfloat16 [8, 1024, 1024], P('dp', 'seq'), may hold values from -6 to 6
Outputs:
- output: bfloat16 [8, 1024, 1024], P('dp', 'seq')
- grad_tokens: float32 [8, 1024, 1024], P('dp', 'seq')
- grad_w_qkv: float32 [1024, 3072], P(('dp', 'seq'))
- grad_w_attn_out: float32 [1024, 1024], P(('dp', 'seq'))
- grad_w_in: float32 [1024, 8192], P(('dp', 'seq'))
- grad_w_down: float32 [4096, 1024], P(('dp', 'seq'))
- grad_s_qk: float32 [1024], P(('dp', 'seq'))
- grad_s_u: float32 [4096], P(('dp', 'seq'))
- grad_s_v: float32 [4096], P(('dp', 'seq'))
- grad_alpha_attn: float32 [1024], P(('dp', 'seq'))
- grad_alpha_mlp: float32 [1024], P(('dp', 'seq'))
Inputs may be any that keep to these rules, and one draw needn't show every extreme that they name: `segments`: in each sequence ids count documents from 1 at the first token and rise by one at each new document; documents hold 200 to 2000 tokens except where a sequence's end cuts one; each sequence ends in 1 to 199 padding tokens of id 0; in one sequence of each draw every whole document holds exactly 200 tokens and one padding token ends it.
All inputs are finite; a program needn't handle non-finite values.
Results may differ from a plain program's by a relative error of at most 0.019.
Values may be sent and summed in bfloat16 or wider, within the bound.
A program may use at most 192 MiB of HBM per device.

v0:
```python
import math
import jax
import jax.numpy as jnp
from jax import lax
from jax.sharding import PartitionSpec as P

HEADS = 16
HD = 64
EPS = 1e-06
ROPE_BASE = 10000.0
MASKED_SCORE = -1e30


def as_sent(array):

    def short(part):
        return part.astype(jnp.bfloat16) if part.dtype == jnp.float32 else part

    return jax.tree.map(short, array)


def rms_norm(values):
    inverse = lax.rsqrt(jnp.mean(values * values, axis=-1, keepdims=True) + EPS)
    return (values * inverse, inverse)


def rms_back(grad_in, normed, inverse):
    return inverse * (grad_in - normed * jnp.mean(grad_in * normed, axis=-1, keepdims=True))


def contract_rows(left_arr, right_arr):
    return lax.dot_general(
        left_arr, right_arr, (((0,), (0,)), ((), ())), preferred_element_type=jnp.float32
    )


def contract_cols(left_arr, right_arr):
    return lax.dot_general(
        left_arr, right_arr, (((1,), (1,)), ((), ())), preferred_element_type=jnp.float32
    )


def doc_positions(seg_row):
    length = seg_row.shape[0]
    places = jnp.arange(length, dtype=jnp.int32)
    is_start = jnp.concatenate([jnp.ones((1,), dtype=bool), seg_row[1:] != seg_row[:-1]])
    starts = lax.cummax(jnp.where(is_start, places, 0), axis=0)
    return (places - starts).astype(jnp.float32)


def rope_tables(positions, head_dim):
    half_dim = head_dim // 2
    inverse_freq = ROPE_BASE ** (-(jnp.arange(half_dim, dtype=jnp.float32) * 2.0 / head_dim))
    angles = positions[:, None] * inverse_freq[None, :]
    return (jnp.cos(angles)[:, None, :], jnp.sin(angles)[:, None, :])


def rotate(values, cosine, sine_tab):
    half_dim = values.shape[-1] // 2
    low_half = values[..., :half_dim]
    high_half = values[..., half_dim:]
    return jnp.concatenate(
        [low_half * cosine - high_half * sine_tab, high_half * cosine + low_half * sine_tab],
        axis=-1,
    )


def head_prep(head_raw, cosine, sine_tab, head_gain):
    rotated = rotate(head_raw.astype(jnp.float32), cosine, sine_tab)
    head_unit, inverse = rms_norm(rotated)
    return (head_unit, inverse, (head_unit * head_gain).astype(jnp.bfloat16))


def head_back(grad_n, head_unit, inverse, head_gain, cosine, sine_tab):
    grad_rot = rms_back(grad_n * head_gain, head_unit, inverse)
    return rotate(grad_rot, cosine, -sine_tab)


def allowed(seg_row, block_start, block_len):
    query_idx = block_start + jnp.arange(block_len, dtype=jnp.int32)
    key_idx = jnp.arange(seg_row.shape[0], dtype=jnp.int32)
    seg_query = lax.dynamic_slice_in_dim(seg_row, block_start, block_len)
    same_doc = seg_query[:, None] == seg_row[None, :]
    causal = key_idx[None, :] <= query_idx[:, None]
    not_padding = (seg_query[:, None] != 0) | (key_idx[None, :] == query_idx[:, None])
    return causal & same_doc & not_padding


def attend_forward(query_n, key_n, value_b, seg_row, score_scale):
    length, groups, head_dim = query_n.shape
    block_len = min(512, length)
    block_count = length // block_len
    query_blocks = query_n.reshape(block_count, block_len, groups, head_dim)
    starts = jnp.arange(block_count, dtype=jnp.int32) * block_len

    def one_block(block_in):
        query_part, block_start = block_in
        scores = (
            jnp.einsum("qhd,khd->hqk", query_part, key_n, preferred_element_type=jnp.float32)
            * score_scale
        )
        mask_ok = allowed(seg_row, block_start, block_len)
        scores = jnp.where(mask_ok[None], scores, MASKED_SCORE)
        row_max = jnp.max(scores, axis=-1, keepdims=True)
        weights_exp = jnp.exp(scores - row_max)
        row_total = jnp.sum(weights_exp, axis=-1, keepdims=True)
        attn_probs = (weights_exp / row_total).astype(jnp.bfloat16)
        attn_part = jnp.einsum(
            "hqk,khd->qhd", attn_probs, value_b, preferred_element_type=jnp.float32
        )
        return (attn_part.astype(jnp.bfloat16), (row_max + jnp.log(row_total))[..., 0])

    attn_mixed, log_sums = lax.map(one_block, (query_blocks, starts))
    return (attn_mixed.reshape(length, groups * head_dim), log_sums)


def attend_backward(query_n, key_n, value_b, grad_attn, log_sums, seg_row, score_scale):
    length, groups, head_dim = query_n.shape
    block_len = min(512, length)
    block_count = length // block_len
    query_blocks = query_n.reshape(block_count, block_len, groups, head_dim)
    grad_blocks = grad_attn.reshape(block_count, block_len, groups, head_dim)
    starts = jnp.arange(block_count, dtype=jnp.int32) * block_len

    def one_block(accums, block_in):
        key_acc, value_acc = accums
        query_part, grad_part, lse_part, block_start = block_in
        scores = (
            jnp.einsum("qhd,khd->hqk", query_part, key_n, preferred_element_type=jnp.float32)
            * score_scale
        )
        mask_ok = allowed(seg_row, block_start, block_len)
        attn_probs = jnp.where(mask_ok[None], jnp.exp(scores - lse_part[..., None]), 0.0)
        grad_probs = jnp.einsum(
            "qhd,khd->hqk", grad_part, value_b, preferred_element_type=jnp.float32
        )
        delta_row = jnp.sum(grad_probs * attn_probs, axis=-1, keepdims=True)
        grad_scores = (attn_probs * (grad_probs - delta_row)).astype(jnp.bfloat16)
        grad_query = (
            jnp.einsum("hqk,khd->qhd", grad_scores, key_n, preferred_element_type=jnp.float32)
            * score_scale
        )
        key_acc = (
            key_acc
            + jnp.einsum(
                "hqk,qhd->khd", grad_scores, query_part, preferred_element_type=jnp.float32
            )
            * score_scale
        )
        value_acc = value_acc + jnp.einsum(
            "hqk,qhd->khd",
            attn_probs.astype(jnp.bfloat16),
            grad_part,
            preferred_element_type=jnp.float32,
        )
        return ((key_acc, value_acc), grad_query)

    zeros_init = jnp.zeros((length, groups, head_dim), jnp.float32)
    (grad_key, grad_value), grad_query = lax.scan(
        one_block, (zeros_init, zeros_init), (query_blocks, grad_blocks, log_sums, starts)
    )
    return (grad_query.reshape(length, groups, head_dim), grad_key, grad_value)


def body(
    tokens,
    segments,
    w_qkv,
    w_attn_out,
    w_in,
    w_down,
    s_qk,
    s_u,
    s_v,
    alpha_attn,
    alpha_mlp,
    cotangent,
):
    model_width = tokens.shape[-1]
    inputs_b = tokens.reshape(-1, model_width)
    inputs_f = inputs_b.astype(jnp.float32)
    seg_row = segments.reshape(-1)
    seq_count = lax.axis_size("seq")
    dp_count = lax.axis_size("dp")
    head_group = HEADS // seq_count
    group_width = head_group * HD
    offset = lax.axis_index("seq") * group_width
    head_gain = lax.dynamic_slice_in_dim(s_qk, offset, group_width).reshape(head_group, HD)
    score_scale = 1.0 / math.sqrt(HD)
    full_qkv, full_out, full_in, full_down = (
        lax.all_gather(w_qkv, "dp", axis=0, tiled=True),
        lax.all_gather(w_attn_out, "dp", axis=0, tiled=True),
        lax.all_gather(w_in, "dp", axis=0, tiled=True),
        lax.all_gather(w_down, "dp", axis=0, tiled=True),
    )
    projected = jnp.dot(inputs_b, full_qkv, preferred_element_type=jnp.float32).astype(jnp.bfloat16)
    by_heads = lax.all_to_all(
        projected.reshape(-1, 3, model_width), "seq", split_axis=2, concat_axis=0, tiled=True
    )
    length = by_heads.shape[0]
    cosine, sine_tab = rope_tables(doc_positions(seg_row), HD)
    query_unit, query_inv, query_n = head_prep(
        by_heads[:, 0].reshape(length, head_group, HD), cosine, sine_tab, head_gain
    )
    key_unit, key_inv, key_n = head_prep(
        by_heads[:, 1].reshape(length, head_group, HD), cosine, sine_tab, head_gain
    )
    value_b = by_heads[:, 2].reshape(length, head_group, HD)
    attn_mixed, log_sums = attend_forward(query_n, key_n, value_b, seg_row, score_scale)
    attn_pieces = lax.all_to_all(attn_mixed, "seq", split_axis=0, concat_axis=1, tiled=True)
    attn_proj = jnp.dot(attn_pieces, full_out, preferred_element_type=jnp.float32)
    attn_unit, attn_inv = rms_norm(attn_proj)
    hidden, hidden_inv = rms_norm(inputs_f + alpha_attn * (attn_unit - inputs_f))
    hidden_b = hidden.astype(jnp.bfloat16)
    up_gate = jnp.dot(hidden_b, full_in, preferred_element_type=jnp.float32)
    ff_width = s_u.shape[0]
    up_raw = up_gate[:, :ff_width]
    gate_raw = up_gate[:, ff_width:]
    up_val = s_u * up_raw
    gate_val = s_v * gate_raw
    gate_sig = jax.nn.sigmoid(gate_val)
    silu_gate = gate_val * gate_sig
    inner_act = (silu_gate * up_val).astype(jnp.bfloat16)
    down_proj = jnp.dot(inner_act, full_down, preferred_element_type=jnp.float32)
    mlp_unit, mlp_inv = rms_norm(down_proj)
    result, result_inv = rms_norm(hidden + alpha_mlp * (mlp_unit - hidden))
    output = result.astype(jnp.bfloat16).reshape(tokens.shape)
    grad_res = cotangent.reshape(-1, model_width).astype(jnp.float32)
    grad_two = rms_back(grad_res, result, result_inv)
    grad_alpha_mlp = jnp.sum(grad_two * (mlp_unit - hidden), axis=0)
    grad_down_proj = rms_back(alpha_mlp * grad_two, mlp_unit, mlp_inv).astype(jnp.bfloat16)
    grad_w_down = contract_rows(inner_act, grad_down_proj)
    grad_inner = contract_cols(grad_down_proj, full_down)
    grad_up_val = grad_inner * silu_gate
    grad_gate_val = grad_inner * up_val * gate_sig * (1.0 + gate_val * (1.0 - gate_sig))
    grad_s_u = jnp.sum(grad_up_val * up_raw, axis=0)
    grad_s_v = jnp.sum(grad_gate_val * gate_raw, axis=0)
    grad_up_gate = jnp.concatenate([grad_up_val * s_u, grad_gate_val * s_v], axis=1).astype(
        jnp.bfloat16
    )
    grad_w_in = contract_rows(hidden_b, grad_up_gate)
    grad_hidden = (1.0 - alpha_mlp) * grad_two + contract_cols(grad_up_gate, full_in)
    grad_one = rms_back(grad_hidden, hidden, hidden_inv)
    grad_alpha_attn = jnp.sum(grad_one * (attn_unit - inputs_f), axis=0)
    grad_attn_proj = rms_back(alpha_attn * grad_one, attn_unit, attn_inv).astype(jnp.bfloat16)
    grad_w_attn_out = contract_rows(attn_pieces, grad_attn_proj)
    grad_pieces = contract_cols(grad_attn_proj, full_out).astype(jnp.bfloat16)
    grad_heads = lax.all_to_all(
        grad_pieces, "seq", split_axis=1, concat_axis=0, tiled=True
    ).reshape(length, head_group, HD)
    grad_query_n, grad_key_n, grad_value = attend_backward(
        query_n, key_n, value_b, grad_heads, log_sums, seg_row, score_scale
    )
    grad_head_gain = jnp.sum(grad_query_n * query_unit + grad_key_n * key_unit, axis=0)
    grad_query = head_back(grad_query_n, query_unit, query_inv, head_gain, cosine, sine_tab)
    grad_key = head_back(grad_key_n, key_unit, key_inv, head_gain, cosine, sine_tab)
    grad_stack = (
        jnp.stack([grad_query, grad_key, grad_value], axis=1)
        .reshape(length, 3, group_width)
        .astype(jnp.bfloat16)
    )
    grad_qkv = lax.all_to_all(grad_stack, "seq", split_axis=0, concat_axis=2, tiled=True).reshape(
        -1, 3 * model_width
    )
    grad_w_qkv = contract_rows(inputs_b, grad_qkv)
    grad_inputs = (1.0 - alpha_attn) * grad_one + contract_cols(grad_qkv, full_qkv)
    grad_s_qk = lax.dynamic_update_slice_in_dim(
        jnp.zeros((model_width,), jnp.float32), grad_head_gain.reshape(-1), offset, 0
    )
    grad_terms = (
        grad_w_qkv,
        grad_w_attn_out,
        grad_w_in,
        grad_w_down,
        grad_s_qk,
        grad_s_u,
        grad_s_v,
        grad_alpha_attn,
        grad_alpha_mlp,
    )
    shaped = tuple(
        (
            term_arr.reshape(
                (dp_count, seq_count, term_arr.shape[0] // (dp_count * seq_count))
                + term_arr.shape[1:]
            )
            for term_arr in grad_terms
        )
    )
    within = jax.tree.map(
        lambda part: part.astype(jnp.float32),
        lax.psum_scatter(as_sent(shaped), "seq", scatter_dimension=1, tiled=True),
    )
    across = jax.tree.map(
        lambda part: part.astype(jnp.float32),
        lax.psum_scatter(as_sent(within), "dp", scatter_dimension=0, tiled=True),
    )
    shards = tuple((term_arr.reshape(term_arr.shape[2:]) for term_arr in across))
    return (output, grad_inputs.reshape(tokens.shape)) + tuple(shards)


def solution(mesh):
    placed = (
        P("dp", "seq", None),
        P("dp", None),
        P("dp", None),
        P("dp", None),
        P("dp", None),
        P("dp", None),
        P(),
        P(),
        P(),
        P(),
        P(),
        P("dp", "seq", None),
    )
    return jax.shard_map(
        body,
        mesh=mesh,
        in_specs=placed,
        out_specs=(
            P("dp", "seq", None),
            P("dp", "seq", None),
            P(("dp", "seq"), None),
            P(("dp", "seq"), None),
            P(("dp", "seq"), None),
            P(("dp", "seq"), None),
            P(("dp", "seq")),
            P(("dp", "seq")),
            P(("dp", "seq")),
            P(("dp", "seq")),
            P(("dp", "seq")),
        ),
        check_vma=False,
    )
```

profile of v0, /device:TPU:0, one launch (start us, length us, event | category | flops | bytes accessed | tf_op | source)
XLA Modules:
  0.0 1722.5 jit_solution(12970683820882381391)
XLA Ops:
  9.4 48.6 %all-gather.5.cloned.1.call-done = bf16[1024,3072]{1,0:T(8,128)(2,1)} async-done(((bf16[128,3072]{1,0:T(8,128)(2,1)}), bf16[1024,3072]{1,0:T(8,128)(2,1)}) %all-gather.5.cloned.1.call-update) | async-done | bytes 6291472 | tf_op jit(solution)/shard_map/all_gather | solution.py:191
  58.0 4.8 convolution_convert_fusion.3
  63.5 2.7 copy.92
  66.2 4.6 all-to-all-start
  74.2 45.2 %all-to-all-done = bf16[256,3,1024]{0,1,2:T(4,128)(2,1)S(1)} async-done(((bf16[256,3,1024]{0,1,2:T(4,128)(2,1)}), bf16[256,3,1024]{0,1,2:T(4,128)(2,1)S(1)}, u32[]{:S(2)}, u32[]{:S(2)}) %all-to-all-start) | async-done | bytes 1572896 | tf_op jit(solution)/shard_map/all_to_all | solution.py:197
  124.7 2.5 copy.96
  128.6 2.0 multiply_subtract_fusion.1
  135.9 27.1 %while.27 = (s32[]{:T(128)}, bf16[2,512,4,64]{1,3,2,0:T(8,128)(2,1)}, f32[2,4,512]{2,1,0:T(4,128)S(1)}, s32[2]{0:T(128)S(1)}, s32[1024]{0:T(1024)S(1)}, /*index=...) while((s32[]{:T(128)}, ...), condition=%wide.region_7.8_spmd, body=%wide.region_4.7_spmd.sunk | while | flops 565312512 | bytes 33111288 | solution.py:113
  140.0 2.6 fusion.121
  142.7 2.3 fusion.122
  145.0 3.7 fusion.123
  153.6 2.6 fusion.121
  156.2 2.3 fusion.122
  158.6 3.7 fusion.123
  165.7 3.7 all-to-all-start.1
  169.5 13.9 all-to-all-done.1
  183.4 2.6 multiply_reduce_fusion.13
  187.5 9.0 fusion.72
  196.5 3.2 copy-done
  199.7 2.3 multiply_convert_fusion.3
  202.0 33.4 %all-gather.11.cloned.1.call-done = bf16[4096,1024]{1,0:T(8,128)(2,1)} async-done(((bf16[512,1024]{1,0:T(8,128)(2,1)}), bf16[4096,1024]{1,0:T(8,128)(2,1)}) %all-gather.11.cloned.1.call-update) | async-done | bytes 8388624 | tf_op jit(solution)/shard_map/all_gather | solution.py:194
  235.4 6.5 multiply_reduce_fusion.11
  245.9 9.2 multiply_reduce_fusion.1
  256.8 12.7 multiply_reduce_fusion.8
  269.6 2.9 multiply_reduce_fusion.4
  275.4 4.8 all-to-all-start.2
  280.2 14.9 all-to-all-done.2
  296.3 1.9 reshape_reshape.3
  299.0 62.1 %while.28 = (s32[]{:T(128)}, f32[1024,4,64]{0,2,1:T(8,128)S(1)}, f32[1024,4,64]{0,2,1:T(8,128)}, f32[2,512,4,64]{1,0,3,2:T(2,128)}, bf16[2,512,4,64]{1,3,2,0:T(8...) while((s32[]{:T(128)}, f32[1024,4,64]{0,2,1:T(8,128)S(1)}, ...), condition=%wide.region_18.19_spmd.clone, body=%wide.region_16.18_spmd.clone.sunk | while | flops 1378221056 | bytes 82910512 | solution.py:159
  303.1 2.3 fusion.133
  305.5 3.1 fusion.136
  308.6 4.8 multiply_reduce_fusion.17
  313.4 2.4 multiply_convert_fusion.13
  317.2 1.9 fusion.135
  319.7 10.4 dynamic_update_slice.24
  334.2 2.3 fusion.133
  336.5 3.1 fusion.136
  339.7 4.8 multiply_reduce_fusion.17
  344.4 2.4 multiply_convert_fusion.13
  348.2 1.9 fusion.135
  350.7 10.4 dynamic_update_slice.24
  361.2 2.4 multiply_reduce_fusion.6
  363.6 3.1 reshape.556
  368.1 2.2 add_reduce_fusion
  371.1 2.6 copy.107
  373.8 4.6 all-to-all-start.3
  378.4 2.1 convolution_convert_fusion.4
  380.5 7.2 convolution_convert_fusion.1
  387.7 10.4 convolution_convert_fusion
  398.2 28.0 %all-to-all-done.3 = bf16[1024,3,256]{2,1,0:T(4,128)(2,1)} async-done(((bf16[1024,3,256]{2,1,0:T(4,128)(2,1)}), bf16[1024,3,256]{2,1,0:T(4,128)(2,1)}, u32[]{:S(2)}, u32[]{:S(2)}) %all-to-all-start.3) | async-done | bytes 1572896 | tf_op jit(solution)/shard_map/all_to_all | solution.py:262
  426.2 1.8 copy.108
  428.7 5.5 convolution_convert_fusion.2
  435.5 1101.0 %all-reduce.19.cloned.1.call-done = (bf16[8,4,32,3072]{3,2,1,0:T(8,128)(2,1)}, bf16[8,4,32,1024]{3,2,1,0:T(8,128)(2,1)}, bf16[8,4,32,8192]{3,2,1,0:T(8,128)(2,1)}, bf16[8,4,128,1024]{3,2,1,0:T(8,128)(2,1)}) async-done(((bf16[8,4,32,3072]{3,2,1,0:T(8,128)(2,1)}, bf16[8,4,32,1024]{3,2,1,0:T(8,128)(2,1)}, bf16[8,4,32,8192]{3,2,1,0:T(8,128)(2,1)}, bf16[8,4,128,1024]{3,2,1,0:T(8,128)(2,1)}), ...) | async-done | bytes 33554448
  1536.4 2.5 constant_dynamic-slice_fusion.12
  1539.0 3.3 constant_dynamic-slice_fusion.13
  1542.4 3.8 constant_dynamic-slice_fusion.10
  1546.5 5.3 constant_dynamic-slice_fusion.11
  1553.7 16.8 all-reduce.15
  1573.8 22.4 %all-reduce.14 = (bf16[8,1,32]{2,1,0:T(2,128)(2,1)S(1)}, bf16[8,1,128]{2,1,0:T(2,128)(2,1)S(1)}, bf16[8,1,128]{2,1,0:T(2,128)(2,1)S(1)}, bf16[8,1,32]{2,1,0:T(2,128)(2,1)S(1)}, bf16[8,1,32]{2,1,0:T(2,128)(2,1)S(1)}) all-reduce(bf16[8,1,32]{2,1,0:T(2,128)(2,1)S(1)} %copy.111, ...), channel_id=11, replica_groups=mesh['dp'=8,'seq'=4] {'dp'}, use_global_device_ids=true, to_apply=%region_31.32.clone | all-reduce | flops 2816 | bytes 11264
  1602.0 5.7 fusion.50
  1609.2 5.4 reduce-scatter.17.cloned.1.call-done
  1616.3 42.7 %reduce-scatter.23.cloned.1.call-done = bf16[1,1,128,1024]{3,2,1,0:T(8,128)(2,1)} async-done(((bf16[8,1,128,1024]{3,2,1,0:T(8,128)(2,1)}), bf16[1,1,128,1024]{3,2,1,0:T(8,128)(2,1)}) %reduce-scatter.23.cloned.1.call-update) | async-done | bytes 262160 | tf_op jit(solution)/shard_map/reduce_scatter | solution.py:296
  1660.8 52.8 %reduce-scatter.21.cloned.1.call-done = bf16[1,1,32,8192]{3,2,1,0:T(8,128)(2,1)} async-done(((bf16[8,1,32,8192]{3,2,1,0:T(8,128)(2,1)}), bf16[1,1,32,8192]{3,2,1,0:T(8,128)(2,1)}) %reduce-scatter.21.cloned.1.call-update) | async-done | bytes 524304 | tf_op jit(solution)/shard_map/reduce_scatter | solution.py:296
  1713.6 2.1 bitcast_convert_fusion
  (247 shorter events, 67.4 us)
Async XLA Ops:
  7.2 50.8 %all-gather.5.cloned.1.call-start = ((), (), s32[]{:S(2)}) async-start(), calls=%async_computation.8 | async-start | bytes 7077888 | tf_op jit(solution)/shard_map/all_gather | solution.py:191
  7.9 161.6 %all-gather.7.cloned.1.call-start = ((), (), s32[]{:S(2)}) async-start(), calls=%async_computation.9 | async-start | bytes 2359296 | tf_op jit(solution)/shard_map/all_gather | solution.py:192
  8.7 178.8 %all-gather.9.cloned.1.call-start = ((), (), s32[]{:S(2)}) async-start(), calls=%async_computation.10 | async-start | bytes 18874368 | tf_op jit(solution)/shard_map/all_gather | solution.py:193
  63.5 8.8 copy-start.22
  66.2 53.2 %all-to-all-start = ((bf16[256,3,1024]{0,1,2:T(4,128)(2,1)}), bf16[256,3,1024]{0,1,2:T(4,128)(2,1)S(1)}, u32[]{:S(2)}, u32[]{:S(2)}) async-start(bf16[256,3,1024]{0,1,2:T(4,128)(2,1)} %copy.92), calls=%async_computation | async-start | bytes 4194304 | tf_op jit(solution)/shard_map/all_to_all | solution.py:197
  70.8 164.6 %all-gather.11.cloned.1.call-start = ((), (), s32[]{:S(2)}) async-start(), calls=%async_computation.11 | async-start | bytes 9437184 | tf_op jit(solution)/shard_map/all_gather | solution.py:194
  72.3 61.1 %copy-start.36 = (f32[4,64]{1,0:T(4,128)}, f32[4,64]{1,0:T(4,128)S(1)}, u32[]{:S(2)}) copy-start(f32[4,64]{1,0:T(4,128)S(1)} %mul.496) | copy-start | bytes 3076
  74.2 54.3 %copy-start.23 = (f32[1024,32]{0,1:T(8,128)}, f32[1024,32]{0,1:T(8,128)S(1)}, u32[]{:S(2)}) copy-start(f32[1024,32]{0,1:T(8,128)S(1)} %get-tuple-element.371) | copy-start | bytes 393220
  130.5 5.4 copy-start.4
  130.5 5.4 copy-start.6
  130.5 5.4 copy-start.8
  130.6 5.3 copy-start.9
  131.0 4.9 copy-start.11
  133.3 2.6 copy-start.34
  133.4 2.6 copy-start.32
  142.7 2.4 copy-start.27
  148.7 0.8 copy-start.28
  156.2 2.4 copy-start.27
  162.2 0.8 copy-start.28
  163.0 6.4 copy-start.39
  163.0 23.9 %copy-start.10 = (bf16[1,256,1024]{2,1,0:T(8,128)(2,1)S(1)}, bf16[1,256,1024]{2,1,0:T(8,128)(2,1)}, u32[]{:S(2)}) copy-start(bf16[1,256,1024]{2,1,0:T(8,128)(2,1)} %param.16) | copy-start | bytes 1572868
  163.0 23.9 %copy-start.40 = (f32[1024]{0:T(1024)S(1)}, f32[1024]{0:T(1024)}, u32[]{:S(2)}) copy-start(f32[1024]{0:T(1024)} %param.25) | copy-start | bytes 12292
  165.7 17.6 %all-to-all-start.1 = ((bf16[4,256,256]{1,2,0:T(8,128)(2,1)}), bf16[4,256,256]{1,2,0:T(8,128)(2,1)S(1)}, u32[]{:S(2)}, u32[]{:S(2)}) async-start(bf16[4,256,256]{1,2,0:T(8,128)(2,1)} %copy.100), calls=%async_computation.1 | async-start | bytes 1048576 | tf_op jit(solution)/shard_map/all_to_all | solution.py:210
  183.4 2.6 copy-start.13
  186.0 1.0 copy-start.2
  187.5 12.3 copy-start.38
  187.5 12.3 copy-start.42
  196.5 3.2 copy-start
  235.4 7.0 copy-start.12
  242.4 3.6 copy-start.1
  245.0 10.1 copy-start.17
  269.6 2.9 copy-start.3
  269.6 4.0 copy-start.19
  272.4 7.8 copy-start.15
  272.7 0.9 copy-start.20
  275.4 19.7 %all-to-all-start.2 = ((bf16[256,4,256]{0,2,1:T(8,128)(2,1)}), bf16[256,4,256]{0,2,1:T(8,128)(2,1)S(1)}, u32[]{:S(2)}, u32[]{:S(2)}) async-start(bf16[256,4,256]{0,2,1:T(8,128)(2,1)} %bitcast.275), calls=%async_computation.2 | async-start | bytes 1048576 | tf_op jit(solution)/shard_map/all_to_all | solution.py:248
  299.0 62.1 %copy-start.33 = (f32[2,512,4]{1,0,2:T(2,128)S(1)}, f32[2,512,4]{1,0,2:T(2,128)}, u32[]{:S(2)}) copy-start(f32[2,512,4]{1,0,2:T(2,128)} %copy-done.32) | copy-start | bytes 49156
  299.0 62.1 %copy-start.37 = (f32[4,64]{1,0:T(4,128)S(1)}, f32[4,64]{1,0:T(4,128)}, u32[]{:S(2)}) copy-start(f32[4,64]{1,0:T(4,128)} %copy-done.36) | copy-start | bytes 3076
  303.1 2.3 copy-start.25
  308.6 4.8 copy-start.26
  334.2 2.3 copy-start.25
  339.6 4.8 copy-start.26
  361.1 6.9 copy-start.5
  361.1 6.9 copy-start.7
  361.1 6.9 copy-start.31
  361.1 6.9 copy-start.35
  368.0 2.5 copy-start.24
  368.0 2.5 copy-start.29
  371.1 7.3 copy-start.14
  373.8 4.7 copy-start.21
  373.8 6.7 copy-start.18
  373.8 52.4 %all-to-all-start.3 = ((bf16[1024,3,256]{2,1,0:T(4,128)(2,1)}), bf16[1024,3,256]{2,1,0:T(4,128)(2,1)}, u32[]{:S(2)}, u32[]{:S(2)}) async-start(bf16[1024,3,256]{2,1,0:T(4,128)(2,1)} %copy.107), calls=%async_computation.3 | async-start | bytes 4194304 | tf_op jit(solution)/shard_map/all_to_all | solution.py:262
  378.4 1158.0 %all-reduce.19.cloned.1.call-start = ((), (), s32[]{:S(2)}) async-start(), calls=%async_computation.16 | async-start | bytes 67108864
  434.2 0.7 copy-start.48
  434.2 1173.5 %reduce-scatter.19.cloned.1.call-start = ((), (), s32[]{:S(2)}) async-start(), calls=%async_computation.13 | async-start | bytes 589824 | tf_op jit(solution)/shard_map/reduce_scatter | solution.py:296
  1539.0 75.7 %reduce-scatter.17.cloned.1.call-start = ((), (), s32[]{:S(2)}) async-start(), calls=%async_computation.12 | async-start | bytes 1769472 | tf_op jit(solution)/shard_map/reduce_scatter | solution.py:296
  1542.3 116.7 %reduce-scatter.23.cloned.1.call-start = ((), (), s32[]{:S(2)}) async-start(), calls=%async_computation.15 | async-start | bytes 2359296 | tf_op jit(solution)/shard_map/reduce_scatter | solution.py:296
  1546.2 167.4 %reduce-scatter.21.cloned.1.call-start = ((), (), s32[]{:S(2)}) async-start(), calls=%async_computation.14 | async-start | bytes 4718592 | tf_op jit(solution)/shard_map/reduce_scatter | solution.py:296
  1551.8 1.2 copy-start.41
  1551.8 1.2 copy-start.46
  1551.8 1.2 copy-start.45
  1551.8 1.3 copy-start.43
  1551.9 1.4 copy-start.44
  1551.9 50.1 %copy-start.16 = (f32[256,1024]{1,0:T(8,128)S(1)}, f32[256,1024]{1,0:T(8,128)}, u32[]{:S(2)}) copy-start(f32[256,1024]{1,0:T(8,128)} %copy-done.15) | copy-start | bytes 3145732
  (2 other events, 1.3 us)
Sparse Core Ops, SparseCore 0:
  9.9 48.1 all-gather.4
  59.9 27.7 all-gather.6
  89.6 89.7 all-gather.8
  181.1 54.2 all-gather.10
  434.4 1102.0 all-reduce.18
  1539.9 33.0 reduce-scatter.18
  1576.3 38.3 reduce-scatter.16
  1617.9 41.0 reduce-scatter.22
  1662.4 51.1 reduce-scatter.20
where the time goes:
time: 1730 us; the launch traced here: 1720 us
  waiting for transfers between devices  1390 us (80%)
  matrix products  116 us (7%)
  local copies, waits for them, and re-layouts  84.5 us (5%)
  other arithmetic  52.8 us (3%)
  blocking collectives  39.2 us (2%)
  starting transfers between devices  18.4 us (1%)
    unnamed x10, waiting for transfers between devices  1100 us
    reduce_scatter x4, waiting for transfers between devices, body(): lax.psum_scatter(as_sent(within), 'dp', scatter_dimension=0, tiled=True)  101 us
    all_gather x1, waiting for transfers between devices, body(): lax.all_gather(w_qkv, 'dp', axis=0, tiled=True)  48.6 us
    all_to_all x1, waiting for transfers between devices, body(): lax.all_to_all(projected.reshape(-1, 3, model_width), 'seq', split_axis=2...  45.2 us
    unnamed x2, blocking collectives  39.2 us
  transfers between devices with their start and end apart: 13, of which 10 were waited for; matrix products, arithmetic and copies ran while one was open for 7% of the time, Pallas kernels for 0%

commit v1 on v0

--- a/solution.py
+++ b/solution.py
@@ -9,6 +9,24 @@
 EPS = 1e-06
 ROPE_BASE = 10000.0
 MASKED_SCORE = -1e30
+
+
+def collect(array, axis, dim):
+    ways, here, step = (lax.axis_size(axis), lax.axis_index(axis), array.shape[dim])
+    shape = [n * ways if d == dim else n for d, n in enumerate(array.shape)]
+    full = lax.dynamic_update_slice_in_dim(
+        jnp.zeros(shape, array.dtype), array, here * step, axis=dim
+    )
+    going_up = going_down = array
+    for far in range(1, ways // 2 + 1):
+        going_up = lax.ppermute(going_up, axis, [(d, (d + 1) % ways) for d in range(ways)])
+        full = lax.dynamic_update_slice_in_dim(full, going_up, (here - far) % ways * step, axis=dim)
+        if 2 * far < ways:
+            going_down = lax.ppermute(going_down, axis, [(d, (d - 1) % ways) for d in range(ways)])
+            full = lax.dynamic_update_slice_in_dim(
+                full, going_down, (here + far) % ways * step, axis=dim
+            )
+    return full
 
 
 def as_sent(array):
@@ -188,7 +206,7 @@
     head_gain = lax.dynamic_slice_in_dim(s_qk, offset, group_width).reshape(head_group, HD)
     score_scale = 1.0 / math.sqrt(HD)
     full_qkv, full_out, full_in, full_down = (
-        lax.all_gather(w_qkv, "dp", axis=0, tiled=True),
+        collect(w_qkv, "dp", 0),
         lax.all_gather(w_attn_out, "dp", axis=0, tiled=True),
         lax.all_gather(w_in, "dp", axis=0, tiled=True),
         lax.all_gather(w_down, "dp", axis=0, tiled=True),

time: 1730 us -> 1740 us (level)
  starting transfers between devices: 18.4 us -> 41 us
  waiting for transfers between devices: 1390 us -> 1370 us
    ppermute x0 -> x7, waiting for transfers between devices: none -> 67.2 us  [the longest x4 63.5 us: collect(): lax.ppermute(going_up, axis, [(d, (d + 1) % ways) for d in range(ways)])]
    all_gather x1 -> x0, waiting for transfers between devices: 48.6 us -> none  [body(): lax.all_gather(w_qkv, 'dp', axis=0, tiled=True)]
    all_gather x1, waiting for transfers between devices: 33.4 us -> 0.01 us  [body(): lax.all_gather(w_down, 'dp', axis=0, tiled=True)]
    ppermute x0 -> x7, starting transfers between devices: none -> 19.1 us  [the longest x4 11.9 us: collect(): lax.ppermute(going_up, axis, [(d, (d + 1) % ways) for d in range(ways)])]
    unnamed x10 -> x9, waiting for transfers between devices: 1100 us -> 1110 us
  transfers between devices with their start and end apart: 13 -> 19, of which waited for: 10 -> 14; matrix products, arithmetic and copies ran while one was open for 7% -> 7% of each run, Pallas kernels for 0% -> 0%
where the time goes in v1:
time: 1740 us
  waiting for transfers between devices  1370 us (79%)
  matrix products  115 us (7%)
  local copies, waits for them, and re-layouts  95.4 us (5%)
  other arithmetic  50.4 us (3%)
  starting transfers between devices  41 us (2%)
  blocking collectives  39.2 us (2%)
    unnamed x9, waiting for transfers between devices  1110 us
    reduce_scatter x4, waiting for transfers between devices, body(): lax.psum_scatter(as_sent(within), 'dp', scatter_dimension=0, tiled=True)  101 us
    ppermute x4, waiting for transfers between devices, collect(): lax.ppermute(going_up, axis, [(d, (d + 1) % ways) for d in range(ways)])  63.5 us
    all_to_all x1, waiting for transfers between devices, body(): lax.all_to_all(projected.reshape(-1, 3, model_width), 'seq', split_axis=2...  40.1 us
    unnamed x2, blocking collectives  39.2 us
  transfers between devices with their start and end apart: 19, of which 14 were waited for; matrix products, arithmetic and copies ran while one was open for 7% of the time, Pallas kernels for 0%

profile of v1, /device:TPU:0, one launch (start us, length us, event | category | flops | bytes accessed | tf_op | source)
XLA Modules:
  0.0 1735.7 jit_solution(18096262606027950302)
XLA Ops:
  9.2 2.9 collective-permute-start.1
  12.2 18.5 %collective-permute-done = bf16[128,3072]{1,0:T(8,128)(2,1)S(1)} collective-permute-done((bf16[128,3072]{1,0:T(8,128)(2,1)}, bf16[128,3072]{1,0:T(8,128)(2,1)S(1)}, u32[]{:S(2)}, u32[]{:S(2)}) %collective-permute-start) | collective-permute-done | bytes 786464 | tf_op jit(solution)/shard_map/ppermute | solution.py:22
  32.2 2.7 collective-permute-start.3
  34.9 3.4 broadcast_in_dim.56
  39.2 15.3 collective-permute-done.2
  60.2 17.8 %collective-permute-done.4 = bf16[128,3072]{1,0:T(8,128)(2,1)S(1)} collective-permute-done((bf16[128,3072]{1,0:T(8,128)(2,1)S(1)}, bf16[128,3072]{1,0:T(8,128)(2,1)S(1)}, u32[]{:S(2)}, u32[]{:S(2)}) %collective-permute-start.4) | collective-permute-done | bytes 786464 | tf_op jit(solution)/shard_map/ppermute | solution.py:22
  78.0 9.4 collective-permute-start.6
  90.4 2.7 collective-permute-done.5
  94.1 12.0 collective-permute-done.6
  107.1 5.1 convolution_convert_fusion.3
  112.2 2.7 copy.75
  114.9 9.0 all-to-all-start
  127.5 40.1 %all-to-all-done = bf16[256,3,1024]{0,1,2:T(4,128)(2,1)S(1)} async-done(((bf16[256,3,1024]{0,1,2:T(4,128)(2,1)}), bf16[256,3,1024]{0,1,2:T(4,128)(2,1)S(1)}, u32[]{:S(2)}, u32[]{:S(2)}) %all-to-all-start) | async-done | bytes 1572896 | tf_op jit(solution)/shard_map/all_to_all | solution.py:215
  167.6 2.7 copy.76
  170.3 2.8 all_to_all.53
  181.2 27.1 %while.27 = (s32[]{:T(128)}, bf16[2,512,4,64]{1,3,2,0:T(8,128)(2,1)}, f32[2,4,512]{2,1,0:T(4,128)S(1)}, s32[2]{0:T(128)S(1)}, s32[1024]{0:T(1024)S(1)}, /*index=...) while((s32[]{:T(128)}, ...), condition=%wide.region_7.8_spmd, body=%wide.region_4.7_spmd.sunk | while | flops 565312512 | bytes 33111288 | solution.py:131
  185.3 2.6 fusion.121
  187.9 2.3 fusion.122
  190.3 3.7 fusion.123
  198.8 2.6 fusion.121
  201.5 2.3 fusion.122
  203.8 3.7 fusion.123
  211.0 3.9 all-to-all-start.1
  215.0 14.1 all-to-all-done.1
  229.1 2.6 multiply_reduce_fusion.13
  233.2 8.2 fusion.72
  241.4 3.2 copy-done
  244.6 2.3 multiply_convert_fusion.3
  246.9 6.5 multiply_reduce_fusion.11
  257.4 8.8 multiply_reduce_fusion.1
  267.9 12.7 multiply_reduce_fusion.8
  280.7 2.9 multiply_reduce_fusion.4
  286.5 3.6 all-to-all-start.2
  290.2 14.0 all-to-all-done.2
  308.2 62.1 %while.28 = (s32[]{:T(128)}, f32[1024,4,64]{0,2,1:T(8,128)S(1)}, f32[1024,4,64]{0,2,1:T(8,128)}, f32[2,512,4,64]{1,0,3,2:T(2,128)}, bf16[2,512,4,64]{1,3,2,0:T(8...) while((s32[]{:T(128)}, f32[1024,4,64]{0,2,1:T(8,128)S(1)}, ...), condition=%wide.region_18.19_spmd.clone, body=%wide.region_16.18_spmd.clone.sunk | while | flops 1378221056 | bytes 82910512 | solution.py:177
  312.3 2.3 fusion.133
  314.6 3.1 fusion.136
  317.7 4.8 multiply_reduce_fusion.17
  322.5 2.4 multiply_convert_fusion.13
  328.8 10.4 dynamic_update_slice.64
  343.3 2.3 fusion.133
  345.7 3.1 fusion.136
  348.8 4.8 multiply_reduce_fusion.17
  353.6 2.4 multiply_convert_fusion.13
  359.9 10.4 dynamic_update_slice.64
  370.3 2.4 multiply_reduce_fusion.6
  372.7 3.1 reshape.556
  380.3 2.6 copy.86
  382.9 4.6 all-to-all-start.3
  389.6 7.2 convolution_convert_fusion.1
  396.8 10.4 convolution_convert_fusion
  407.3 28.0 %all-to-all-done.3 = bf16[1024,3,256]{2,1,0:T(4,128)(2,1)} async-done(((bf16[1024,3,256]{2,1,0:T(4,128)(2,1)}), bf16[1024,3,256]{2,1,0:T(4,128)(2,1)}, u32[]{:S(2)}, u32[]{:S(2)}) %all-to-all-start.3) | async-done | bytes 1572896 | tf_op jit(solution)/shard_map/all_to_all | solution.py:280
  437.8 5.4 convolution_convert_fusion.2
  444.5 1105.0 %all-reduce.19.cloned.1.call-done = (bf16[8,4,32,3072]{3,2,1,0:T(8,128)(2,1)}, bf16[8,4,32,1024]{3,2,1,0:T(8,128)(2,1)}, bf16[8,4,32,8192]{3,2,1,0:T(8,128)(2,1)}, bf16[8,4,128,1024]{3,2,1,0:T(8,128)(2,1)}) async-done(((bf16[8,4,32,3072]{3,2,1,0:T(8,128)(2,1)}, bf16[8,4,32,1024]{3,2,1,0:T(8,128)(2,1)}, bf16[8,4,32,8192]{3,2,1,0:T(8,128)(2,1)}, bf16[8,4,128,1024]{3,2,1,0:T(8,128)(2,1)}), ...) | async-done | bytes 33554448
  1549.5 2.5 constant_dynamic-slice_fusion.12
  1552.1 3.3 constant_dynamic-slice_fusion.13
  1555.4 3.8 constant_dynamic-slice_fusion.10
  1559.5 5.3 constant_dynamic-slice_fusion.11
  1566.6 16.8 all-reduce.15
  1586.8 22.4 %all-reduce.14 = (bf16[8,1,32]{2,1,0:T(2,128)(2,1)S(1)}, bf16[8,1,128]{2,1,0:T(2,128)(2,1)S(1)}, bf16[8,1,128]{2,1,0:T(2,128)(2,1)S(1)}, bf16[8,1,32]{2,1,0:T(2,128)(2,1)S(1)}, bf16[8,1,32]{2,1,0:T(2,128)(2,1)S(1)}) all-reduce(bf16[8,1,32]{2,1,0:T(2,128)(2,1)S(1)} %copy.90, ...), channel_id=11, replica_groups=mesh['dp'=8,'seq'=4] {'dp'}, use_global_device_ids=true, to_apply=%region_31.32.clone | all-reduce | flops 2816 | bytes 11264
  1615.0 5.7 fusion.50
  1622.2 5.4 reduce-scatter.17.cloned.1.call-done
  1629.3 42.7 %reduce-scatter.23.cloned.1.call-done = bf16[1,1,128,1024]{3,2,1,0:T(8,128)(2,1)} async-done(((bf16[8,1,128,1024]{3,2,1,0:T(8,128)(2,1)}), bf16[1,1,128,1024]{3,2,1,0:T(8,128)(2,1)}) %reduce-scatter.23.cloned.1.call-update) | async-done | bytes 262160 | tf_op jit(solution)/shard_map/reduce_scatter | solution.py:314
  1673.8 52.8 %reduce-scatter.21.cloned.1.call-done = bf16[1,1,32,8192]{3,2,1,0:T(8,128)(2,1)} async-done(((bf16[8,1,32,8192]{3,2,1,0:T(8,128)(2,1)}), bf16[1,1,32,8192]{3,2,1,0:T(8,128)(2,1)}) %reduce-scatter.21.cloned.1.call-update) | async-done | bytes 524304 | tf_op jit(solution)/shard_map/reduce_scatter | solution.py:314
  (265 shorter events, 89.8 us)
Async XLA Ops:
  7.2 207.8 %all-gather.4.cloned.1.call-start = ((), (), s32[]{:S(2)}) async-start(), calls=%async_computation.8 | async-start | bytes 2359296 | tf_op jit(solution)/shard_map/all_gather | solution.py:210
  7.9 30.4 %copy-start.26 = (bf16[128,3072]{1,0:T(8,128)(2,1)S(1)}, bf16[128,3072]{1,0:T(8,128)(2,1)}, u32[]{:S(2)}) copy-start(bf16[128,3072]{1,0:T(8,128)(2,1)} %param.18) | copy-start | bytes 2359300
  7.9 225.2 %all-gather.6.cloned.1.call-start = ((), (), s32[]{:S(2)}) async-start(), calls=%async_computation.9 | async-start | bytes 18874368 | tf_op jit(solution)/shard_map/all_gather | solution.py:211
  8.7 21.9 %collective-permute-start = (bf16[128,3072]{1,0:T(8,128)(2,1)}, bf16[128,3072]{1,0:T(8,128)(2,1)S(1)}, u32[]{:S(2)}, u32[]{:S(2)}) collective-permute-start(bf16[128,3072]{1,0:T(8,128)(2,1)} %param.18), channel_id=1, source_target_pairs={{0,4},{4,8},{8,12},{12,16},{16,20},{20,24},{24,28},{28,0},{1,5},{5... | collective-permute-start | bytes 2359304 | tf_op jit(solution)/shard_map/ppermute | solution.py:22
  9.2 23.0 %collective-permute-start.1 = (bf16[128,3072]{1,0:T(8,128)(2,1)}, bf16[128,3072]{1,0:T(8,128)(2,1)S(1)}, u32[]{:S(2)}, u32[]{:S(2)}) collective-permute-start(bf16[128,3072]{1,0:T(8,128)(2,1)} %param.18), channel_id=1, source_target_pairs={{0,28},{4,0},{8,4},{12,8},{16,12},{20,16},{24,20},{28,24},{1,29},{... | collective-permute-start | bytes 2359304 | tf_op jit(solution)/shard_map/ppermute | solution.py:25
  30.6 23.9 %collective-permute-start.2 = (bf16[128,3072]{1,0:T(8,128)(2,1)S(1)}, bf16[128,3072]{1,0:T(8,128)(2,1)S(1)}, u32[]{:S(2)}, u32[]{:S(2)}) collective-permute-start(bf16[128,3072]{1,0:T(8,128)(2,1)S(1)} %collective-permute-done), channel_id=1, source_target_pairs={{0,4},{4,8},{8,12},{12,16},{16,20},{20,24},{24,28},{28,0},{1,5},{5... | collective-permute-start | bytes 2359304 | tf_op jit(solution)/shard_map/ppermute | solution.py:22
  32.2 25.5 %collective-permute-start.3 = (bf16[128,3072]{1,0:T(8,128)(2,1)S(1)}, bf16[128,3072]{1,0:T(8,128)(2,1)}, u32[]{:S(2)}, u32[]{:S(2)}) collective-permute-start(bf16[128,3072]{1,0:T(8,128)(2,1)S(1)} %collective-permute-done.1), channel_id=1, source_target_pairs={{0,28},{4,0},{8,4},{12,8},{16,12},{20,16},{24,20},{28,24},{1,29},{... | collective-permute-start | bytes 2359304 | tf_op jit(solution)/shard_map/ppermute | solution.py:25
  54.5 23.5 %collective-permute-start.4 = (bf16[128,3072]{1,0:T(8,128)(2,1)S(1)}, bf16[128,3072]{1,0:T(8,128)(2,1)S(1)}, u32[]{:S(2)}, u32[]{:S(2)}) collective-permute-start(bf16[128,3072]{1,0:T(8,128)(2,1)S(1)} %collective-permute-done.2), channel_id=1, source_target_pairs={{0,4},{4,8},{8,12},{12,16},{16,20},{20,24},{24,28},{28,0},{1,5},{5... | collective-permute-start | bytes 2359304 | tf_op jit(solution)/shard_map/ppermute | solution.py:22
  57.7 49.4 %copy-start.10 = (bf16[1,256,1024]{2,1,0:T(8,128)(2,1)S(1)}, bf16[1,256,1024]{2,1,0:T(8,128)(2,1)}, u32[]{:S(2)}) copy-start(bf16[1,256,1024]{2,1,0:T(8,128)(2,1)} %param.16) | copy-start | bytes 1572868
  57.7 35.5 %collective-permute-start.5 = (bf16[128,3072]{1,0:T(8,128)(2,1)}, bf16[128,3072]{1,0:T(8,128)(2,1)S(1)}, u32[]{:S(2)}, u32[]{:S(2)}) collective-permute-start(bf16[128,3072]{1,0:T(8,128)(2,1)} %collective-permute-done.3), channel_id=1, source_target_pairs={{0,28},{4,0},{8,4},{12,8},{16,12},{20,16},{24,20},{28,24},{1,29},{... | collective-permute-start | bytes 2359304 | tf_op jit(solution)/shard_map/ppermute | solution.py:25
  78.0 28.2 %collective-permute-start.6 = (bf16[128,3072]{1,0:T(8,128)(2,1)S(1)}, bf16[128,3072]{1,0:T(8,128)(2,1)S(1)}, u32[]{:S(2)}, u32[]{:S(2)}) collective-permute-start(bf16[128,3072]{1,0:T(8,128)(2,1)S(1)} %collective-permute-done.4), channel_id=1, source_target_pairs={{0,4},{4,8},{8,12},{12,16},{16,20},{20,24},{24,28},{28,0},{1,5},{5... | collective-permute-start | bytes 2359304 | tf_op jit(solution)/shard_map/ppermute | solution.py:22
  112.2 13.4 copy-start.21
  114.9 52.7 %all-to-all-start = ((bf16[256,3,1024]{0,1,2:T(4,128)(2,1)}), bf16[256,3,1024]{0,1,2:T(4,128)(2,1)S(1)}, u32[]{:S(2)}, u32[]{:S(2)}) async-start(bf16[256,3,1024]{0,1,2:T(4,128)(2,1)} %copy.75), calls=%async_computation | async-start | bytes 4194304 | tf_op jit(solution)/shard_map/all_to_all | solution.py:215
  123.9 122.9 %all-gather.8.cloned.1.call-start = ((), (), s32[]{:S(2)}) async-start(), calls=%async_computation.10 | async-start | bytes 9437184 | tf_op jit(solution)/shard_map/all_gather | solution.py:212
  125.5 53.0 %copy-start.36 = (f32[4,64]{1,0:T(4,128)}, f32[4,64]{1,0:T(4,128)S(1)}, u32[]{:S(2)}) copy-start(f32[4,64]{1,0:T(4,128)S(1)} %mul.528) | copy-start | bytes 3076
  127.5 46.8 %copy-start.22 = (f32[1024,32]{0,1:T(8,128)}, f32[1024,32]{0,1:T(8,128)S(1)}, u32[]{:S(2)}) copy-start(f32[1024,32]{0,1:T(8,128)S(1)} %get-tuple-element.371) | copy-start | bytes 393220
  174.7 6.5 copy-start.4
  174.7 6.5 copy-start.6
  174.7 6.5 copy-start.8
  174.7 6.5 copy-start.9
  178.5 2.7 copy-start.34
  178.5 2.6 copy-start.32
  187.9 2.3 copy-start.27
  201.4 2.4 copy-start.27
  208.3 6.6 copy-start.39
  208.3 24.4 %copy-start.40 = (f32[1024]{0:T(1024)S(1)}, f32[1024]{0:T(1024)}, u32[]{:S(2)}) copy-start(f32[1024]{0:T(1024)} %param.25) | copy-start | bytes 12292
  211.0 18.0 %all-to-all-start.1 = ((bf16[4,256,256]{1,2,0:T(8,128)(2,1)}), bf16[4,256,256]{1,2,0:T(8,128)(2,1)S(1)}, u32[]{:S(2)}, u32[]{:S(2)}) async-start(bf16[4,256,256]{1,2,0:T(8,128)(2,1)} %copy.79), calls=%async_computation.1 | async-start | bytes 1048576 | tf_op jit(solution)/shard_map/all_to_all | solution.py:228
  229.1 2.6 copy-start.12
  233.1 11.4 copy-start.38
  233.2 11.4 copy-start.42
  241.4 3.2 copy-start
  246.9 7.0 copy-start.11
  253.8 3.6 copy-start.1
  256.5 9.7 copy-start.16
  280.7 2.9 copy-start.3
  280.7 4.1 copy-start.18
  283.6 6.6 copy-start.14
  286.5 17.7 %all-to-all-start.2 = ((bf16[256,4,256]{0,2,1:T(8,128)(2,1)}), bf16[256,4,256]{0,2,1:T(8,128)(2,1)S(1)}, u32[]{:S(2)}, u32[]{:S(2)}) async-start(bf16[256,4,256]{0,2,1:T(8,128)(2,1)} %bitcast.276), calls=%async_computation.2 | async-start | bytes 1048576 | tf_op jit(solution)/shard_map/all_to_all | solution.py:266
  308.2 62.1 %copy-start.33 = (f32[2,512,4]{1,0,2:T(2,128)S(1)}, f32[2,512,4]{1,0,2:T(2,128)}, u32[]{:S(2)}) copy-start(f32[2,512,4]{1,0,2:T(2,128)} %copy-done.32) | copy-start | bytes 49156
  308.2 62.1 %copy-start.37 = (f32[4,64]{1,0:T(4,128)S(1)}, f32[4,64]{1,0:T(4,128)}, u32[]{:S(2)}) copy-start(f32[4,64]{1,0:T(4,128)} %copy-done.36) | copy-start | bytes 3076
  312.3 2.3 copy-start.24
  317.7 4.8 copy-start.25
  343.3 2.3 copy-start.24
  348.8 4.8 copy-start.25
  370.3 6.9 copy-start.5
  370.3 6.9 copy-start.7
  370.3 6.9 copy-start.31
  370.3 6.9 copy-start.35
  377.2 2.5 copy-start.23
  377.2 2.5 copy-start.29
  380.3 7.3 copy-start.13
  382.9 4.7 copy-start.20
  382.9 6.7 copy-start.17
  382.9 52.4 %all-to-all-start.3 = ((bf16[1024,3,256]{2,1,0:T(4,128)(2,1)}), bf16[1024,3,256]{2,1,0:T(4,128)(2,1)}, u32[]{:S(2)}, u32[]{:S(2)}) async-start(bf16[1024,3,256]{2,1,0:T(4,128)(2,1)} %copy.86), calls=%async_computation.3 | async-start | bytes 4194304 | tf_op jit(solution)/shard_map/all_to_all | solution.py:280
  387.5 1162.0 %all-reduce.19.cloned.1.call-start = ((), (), s32[]{:S(2)}) async-start(), calls=%async_computation.15 | async-start | bytes 67108864
  443.3 1177.4 %reduce-scatter.19.cloned.1.call-start = ((), (), s32[]{:S(2)}) async-start(), calls=%async_computation.12 | async-start | bytes 589824 | tf_op jit(solution)/shard_map/reduce_scatter | solution.py:314
  1552.0 75.6 %reduce-scatter.17.cloned.1.call-start = ((), (), s32[]{:S(2)}) async-start(), calls=%async_computation.11 | async-start | bytes 1769472 | tf_op jit(solution)/shard_map/reduce_scatter | solution.py:314
  1555.4 116.6 %reduce-scatter.23.cloned.1.call-start = ((), (), s32[]{:S(2)}) async-start(), calls=%async_computation.14 | async-start | bytes 2359296 | tf_op jit(solution)/shard_map/reduce_scatter | solution.py:314
  1559.2 167.3 %reduce-scatter.21.cloned.1.call-start = ((), (), s32[]{:S(2)}) async-start(), calls=%async_computation.13 | async-start | bytes 4718592 | tf_op jit(solution)/shard_map/reduce_scatter | solution.py:314
  1564.8 1.2 copy-start.46
  1564.8 1.2 copy-start.45
  1564.8 1.3 copy-start.43
  1564.8 1.4 copy-start.44
  1564.8 50.1 %copy-start.15 = (f32[256,1024]{1,0:T(8,128)S(1)}, f32[256,1024]{1,0:T(8,128)}, u32[]{:S(2)}) copy-start(f32[256,1024]{1,0:T(8,128)} %copy-done.14) | copy-start | bytes 3145732
  (8 other events, 6.6 us)
Sparse Core Ops, SparseCore 0:
  9.9 38.3 all-gather.3
  50.1 108.6 all-gather.5
  160.7 54.2 all-gather.7
  443.4 1106.0 all-reduce.18
  1553.0 33.0 reduce-scatter.18
  1589.2 38.3 reduce-scatter.16
  1630.9 41.0 reduce-scatter.22
  1675.3 51.1 reduce-scatter.20
